TPU v7x, 32 devices: a whole 2x2x4 slice. The times are simulated.
32 devices in a mesh: dp: 16 (over z, y, core), mp: 2 (over x).
Axes of the slice: x: 2, y: 2, z: 4, core: 2. Of those that a mesh axis runs over, the one named last changes fastest.
Arguments:
- features: bfloat16 [768, 384], P('dp'), may hold values from -100 to 100
- teacher_weight: float32 [384, 131072], P(None, ('dp', 'mp')), may hold values from -250 to 250
- student_weight: float32 [384, 131072], P(None, ('dp', 'mp')), may hold values from -24 to 24
- center: float32 [131072], P(('dp', 'mp')), may hold values from -1 to 1
Outputs:
- blended: float32 [384, 131072], P(None, ('dp', 'mp'))
- new_center: float32 [131072], P(('dp', 'mp'))
- log_targets: float32 [768, 131072], P(None, ('dp', 'mp'))
All inputs are finite; a program needn't handle non-finite values.
Results may differ from a plain program's by a relative error of at most 0.0003.
Values may be sent and summed in bfloat16 or wider, within the bound.
A program may use at most 64 MiB of HBM per device.

v0:
```python
import jax
import jax.numpy as jnp
from jax import lax
from jax.sharding import PartitionSpec as P

ema_momentum = 0.994
center_momentum = 0.9
teacher_temp = 0.07
epsilon = 1e-06


def shards(features, teacher_weight, student_weight, center):
    blended = ema_momentum * teacher_weight + (1.0 - ema_momentum) * student_weight
    col_norm = jnp.sqrt(jnp.sum(blended * blended, axis=0, keepdims=True) + epsilon)
    protos = (blended / col_norm).astype(jnp.bfloat16)
    wide_feats = features.astype(jnp.float32)
    row_norm = jnp.sqrt(jnp.sum(wide_feats * wide_feats, axis=1, keepdims=True) + epsilon)
    unit_rows = (wide_feats / row_norm).astype(jnp.bfloat16)
    images = features.shape[0] * lax.axis_size("dp")
    logits = jnp.dot(
        lax.all_gather(unit_rows, "dp", axis=0, tiled=True),
        protos,
        preferred_element_type=jnp.float32,
    )
    column_sums = jnp.sum(logits, axis=0)
    new_center = center_momentum * center + (1.0 - center_momentum) * (column_sums / images)
    shifted = (logits - new_center[None, :]) / teacher_temp
    totals = lax.psum(jnp.sum(jnp.exp(shifted), axis=1), ("dp", "mp"))
    log_targets = shifted - jnp.log(totals)[:, None]
    return (blended, new_center, log_targets)


def solution(mesh):
    placed = (P("dp", None), P(None, ("dp", "mp")), P(None, ("dp", "mp")), P(("dp", "mp")))
    return jax.shard_map(
        shards,
        mesh=mesh,
        in_specs=placed,
        out_specs=(P(None, ("dp", "mp")), P(("dp", "mp")), P(None, ("dp", "mp"))),
        check_vma=False,
    )
```

profile of v0, /device:TPU:10, one launch (start us, length us, event | category | flops | bytes accessed | tf_op | source)
XLA Modules:
  0.0 98.9 jit_solution(8793507337813024451)
XLA Ops:
  0.6 0.9 fusion.3
  1.5 0.9 fusion.4
  2.4 20.6 %all_gather.3 = bf16[768,384]{1,0:T(8,128)(2,1)S(1)} all-gather(bf16[48,384]{1,0:T(8,128)(2,1)S(1)} %fusion.4), channel_id=1, replica_groups=mesh['dp'=16,'mp'=2] {'dp'}, dimensions={0}, use_global_device_ids=true | all-gather | bytes 626688 | tf_op jit(solution)/shard_map/all_gather | solution.py:21
  22.9 9.3 %multiply_reduce_fusion = (f32[4096]{0:T(1024)S(1)}, f32[384,4096]{1,0:T(8,128)}) fusion(f32[384,4096]{1,0:T(8,128)} %param.6, f32[384,4096]{1,0:T(8,128)} %param.5), kind=kLoop, calls=%fused_computation.4 | loop fusion | flops 7860224 | bytes 18890752 | tf_op jit(solution)/shard_map/reduce_sum | solution.py:14
  32.3 0.0 copy-start.2
  32.3 5.6 %fusion.5 = (f32[4096]{0:T(1024)S(1)}, f32[768,4096]{1,0:T(8,128)S(1)}) fusion(bf16[768,384]{1,0:T(8,128)(2,1)S(1)} %all_gather.3, f32[384,4096]{1,0:T(8,128)} %get-tuple-element.4, f32[4096]{0:T(1024)S(1)} %add_sqrt_fusion), kind=kOutput, calls=%fused_computation.15 | convolution fusion | flops 2422206464 | bytes 19496960 | tf_op jit(solution)/shard_map/dot_general | solution.py:20
  37.9 0.0 copy-start
  37.9 0.0 copy-done.2
  37.9 4.7 %copy-done = f32[768,4096]{1,0:T(8,128)} copy-done((f32[768,4096]{1,0:T(8,128)}, f32[768,4096]{1,0:T(8,128)S(1)}, u32[]{:S(2)}) %copy-start) | copy-done | bytes 12582936
  42.7 0.0 copy-start.1
  42.7 2.2 %exponential_reduce_fusion = f32[768]{0:T(1024)S(1)} fusion(f32[768,4096]{1,0:T(8,128)S(1)} %get-tuple-element.6, f32[4096]{0:T(1024)S(1)} %multiply_add_fusion.1), kind=kLoop, calls=%fused_computation | loop fusion | flops 9436416 | bytes 12602368 | tf_op jit(solution)/shard_map/reduce_sum | solution.py:28
  44.9 41.8 %psum.7 = f32[768]{0:T(1024)S(1)} all-reduce(f32[768]{0:T(1024)S(1)} %exponential_reduce_fusion), channel_id=1, replica_groups=mesh['dp'=16,'mp'=2] {'dp','mp'}, use_global_device_ids=true, to_apply=%region_4.0 | all-reduce | flops 768 | bytes 6144 | tf_op jit(solution)/shard_map/psum | solution.py:28
  86.6 0.0 copy-done.1
  86.6 12.2 %fusion = f32[768,4096]{1,0:T(8,128)} fusion(f32[768,4096]{1,0:T(8,128)} %copy-done, f32[768]{0:T(1024)S(1)} %log.3, f32[4096]{0:T(1024)S(1)} %multiply_add_fusion.1), kind=kLoop, calls=%fused_computation.2 | loop fusion | flops 9437184 | bytes 25185280 | tf_op jit(solution)/shard_map/sub | solution.py:29
  (4 shorter events, 0.0 us)
Async XLA Ops:
  32.3 5.6 %copy-start.2 = (f32[4096]{0:T(1024)S(1)}, f32[4096]{0:T(1024)}, u32[]{:S(2)}) copy-start(f32[4096]{0:T(1024)} %param.7) | copy-start | bytes 49156
  37.9 4.8 %copy-start = (f32[768,4096]{1,0:T(8,128)}, f32[768,4096]{1,0:T(8,128)S(1)}, u32[]{:S(2)}) copy-start(f32[768,4096]{1,0:T(8,128)S(1)} %get-tuple-element.6) | copy-start | bytes 37748740
  42.7 44.0 %copy-start.1 = (f32[4096]{0:T(1024)}, f32[4096]{0:T(1024)S(1)}, u32[]{:S(2)}) copy-start(f32[4096]{0:T(1024)S(1)} %multiply_add_fusion.1) | copy-start | bytes 49156
where the time goes:
time: 99.2 us; the launch traced here: 98.9 us
  blocking collectives  62.3 us (63%)
  other arithmetic  25.5 us (26%)
  matrix products  5.6 us (6%)
  local copies, waits for them, and re-layouts  4.76 us (5%)
    psum x1, blocking collectives, shards(): totals = lax.psum(jnp.sum(jnp.exp(shifted), axis=1), ('dp', 'mp'))  41.8 us
    all_gather x1, blocking collectives, shards(): lax.all_gather(unit_rows, 'dp', axis=0, tiled=True)  20.6 us
    sub x1, other arithmetic, shards(): log_targets = shifted - jnp.log(totals)[:, None]  12.2 us
    reduce_sum x1, other arithmetic, shards(): jnp.sum(blended * blended, axis=0, keepdims=True) + epsilon  9.32 us
    dot_general x1, matrix products, shards(): jnp.dot(lax.all_gather(unit_rows, 'dp', axis=0, tiled=True), protos, pref...  5.6 us
    unnamed x6, local copies, waits for them, and re-layouts  4.76 us
    reduce_sum x1, other arithmetic, shards(): totals = lax.psum(jnp.sum(jnp.exp(shifted), axis=1), ('dp', 'mp'))  2.18 us

commit v1 on v0

--- a/solution.py
+++ b/solution.py
@@ -25,7 +25,9 @@
     column_sums = jnp.sum(logits, axis=0)
     new_center = center_momentum * center + (1.0 - center_momentum) * (column_sums / images)
     shifted = (logits - new_center[None, :]) / teacher_temp
-    totals = lax.psum(jnp.sum(jnp.exp(shifted), axis=1), ("dp", "mp"))
+    x = jnp.sum(jnp.exp(shifted), axis=1)
+    parts = lax.all_gather(x, ("dp", "mp"), axis=0, tiled=False)
+    totals = parts.sum(axis=0)
     log_targets = shifted - jnp.log(totals)[:, None]
     return (blended, new_center, log_targets)
 

time: 99.2 us -> 125 us (1.26)
  the two profiles are of different devices: /device:TPU:10 before, /device:TPU:0 now
where the time goes in v1:
time: 125 us
  blocking collectives  90.1 us (72%)
  other arithmetic  25.6 us (20%)
  matrix products  5.6 us (4%)
  local copies, waits for them, and re-layouts  2.57 us (2%)
    all_gather x1, blocking collectives, shards(): parts = lax.all_gather(x, ('dp', 'mp'), axis=0, tiled=False)  65.3 us
    all_gather x1, blocking collectives, shards(): lax.all_gather(unit_rows, 'dp', axis=0, tiled=True)  24.9 us
    sub x1, other arithmetic, shards(): log_targets = shifted - jnp.log(totals)[:, None]  12.2 us
    reduce_sum x1, other arithmetic, shards(): jnp.sum(blended * blended, axis=0, keepdims=True) + epsilon  9.32 us
    dot_general x1, matrix products, shards(): jnp.dot(lax.all_gather(unit_rows, 'dp', axis=0, tiled=True), protos, pref...  5.6 us
    unnamed x7, local copies, waits for them, and re-layouts  2.57 us

profile of v1, /device:TPU:0, one launch (start us, length us, event | category | flops | bytes accessed | tf_op | source)
XLA Modules:
  0.0 124.6 jit_solution(4416093036752738489)
XLA Ops:
  0.6 0.9 fusion.3
  1.5 0.9 fusion.4
  2.4 24.9 %all_gather.9 = bf16[768,384]{1,0:T(8,128)(2,1)S(1)} all-gather(bf16[48,384]{1,0:T(8,128)(2,1)S(1)} %fusion.4), channel_id=1, replica_groups=mesh['dp'=16,'mp'=2] {'dp'}, dimensions={0}, use_global_device_ids=true | all-gather | bytes 626688 | tf_op jit(solution)/shard_map/all_gather | solution.py:21
  27.3 9.3 %multiply_reduce_fusion = (f32[4096]{0:T(1024)S(1)}, f32[384,4096]{1,0:T(8,128)}) fusion(f32[384,4096]{1,0:T(8,128)} %param.6, f32[384,4096]{1,0:T(8,128)} %param.5), kind=kLoop, calls=%fused_computation.4 | loop fusion | flops 7860224 | bytes 18890752 | tf_op jit(solution)/shard_map/reduce_sum | solution.py:14
  36.6 0.0 copy-start.2
  36.6 5.6 %fusion.5 = (f32[4096]{0:T(1024)S(1)}, f32[768,4096]{1,0:T(8,128)S(1)}) fusion(bf16[768,384]{1,0:T(8,128)(2,1)S(1)} %all_gather.9, f32[384,4096]{1,0:T(8,128)} %get-tuple-element.4, f32[4096]{0:T(1024)S(1)} %add_sqrt_fusion), kind=kOutput, calls=%fused_computation.15 | convolution fusion | flops 2422206464 | bytes 19496960 | tf_op jit(solution)/shard_map/dot_general | solution.py:20
  42.2 0.0 copy-start
  42.2 0.0 copy-done.2
  42.3 0.0 copy-start.1
  42.3 2.2 %exponential_reduce_fusion = f32[768]{0:T(1024)S(1)} fusion(f32[768,4096]{1,0:T(8,128)S(1)} %get-tuple-element.6, f32[4096]{0:T(1024)S(1)} %multiply_add_fusion.1), kind=kLoop, calls=%fused_computation | loop fusion | flops 9436416 | bytes 12602368 | tf_op jit(solution)/shard_map/reduce_sum | solution.py:28
  44.5 2.5 %copy-done = f32[768,4096]{1,0:T(8,128)} copy-done((f32[768,4096]{1,0:T(8,128)}, f32[768,4096]{1,0:T(8,128)S(1)}, u32[]{:S(2)}) %copy-start) | copy-done | bytes 12582936
  47.0 65.3 %all-gather.1 = f32[32,1,768]{2,1,0:T(1,128)S(1)} all-gather(f32[1,1,768]{2,1,0:T(1,128)S(1)} %reshape.23), channel_id=2, replica_groups=mesh['dp'=16,'mp'=2] {'dp','mp'}, dimensions={0}, use_global_device_ids=true | all-gather | bytes 101376 | tf_op jit(solution)/shard_map/all_gather | solution.py:29
  112.3 0.1 reduce_sum.49
  112.4 0.0 copy-done.1
  112.4 12.2 %fusion = f32[768,4096]{1,0:T(8,128)} fusion(f32[768,4096]{1,0:T(8,128)} %copy-done, f32[768]{0:T(1024)S(1)} %log.7, f32[4096]{0:T(1024)S(1)} %multiply_add_fusion.1), kind=kLoop, calls=%fused_computation.2 | loop fusion | flops 9437184 | bytes 25185280 | tf_op jit(solution)/shard_map/sub | solution.py:31
  (5 shorter events, 0.0 us)
Async XLA Ops:
  36.6 5.6 %copy-start.2 = (f32[4096]{0:T(1024)S(1)}, f32[4096]{0:T(1024)}, u32[]{:S(2)}) copy-start(f32[4096]{0:T(1024)} %param.7) | copy-start | bytes 49156
  42.2 4.8 %copy-start = (f32[768,4096]{1,0:T(8,128)}, f32[768,4096]{1,0:T(8,128)S(1)}, u32[]{:S(2)}) copy-start(f32[768,4096]{1,0:T(8,128)S(1)} %get-tuple-element.6) | copy-start | bytes 37748740
  42.3 70.1 %copy-start.1 = (f32[4096]{0:T(1024)}, f32[4096]{0:T(1024)S(1)}, u32[]{:S(2)}) copy-start(f32[4096]{0:T(1024)S(1)} %multiply_add_fusion.1) | copy-start | bytes 49156
